TPU v7x, 32 devices: a whole 2x2x4 slice. The times are simulated.
32 devices in a mesh: seq: 4 (over x, core), head: 8 (over z, y).
Axes of the slice: x: 2, y: 2, z: 4, core: 2. Of those that a mesh axis runs over, the one named last changes fastest.
Arguments:
- queries: bfloat16 [256, 4096], P('seq', 'head'), may hold values from -8 to 8
- new_keys: bfloat16 [256, 256], P('seq'), may hold values from -6 to 6
- new_values: bfloat16 [256, 256], P('seq'), may hold values from -6 to 6
- cache_keys: bfloat16 [3072, 256], P('seq'), may hold values from -8 to 8
- cache_values: bfloat16 [3072, 256], P('seq'), may hold values from -6 to 6
- positions: int32 [256], replicated, may hold values from 0 to 255, each once
- cache_len: int32 [4], replicated, may hold values from 1 to 768, 1920 in all
- out_weight: bfloat16 [4096, 16384], P('head', 'seq'), may hold values from -3.5 to 3.5
Outputs:
- output: float32 [256, 16384], P(None, 'seq')
Inputs may be any that keep to these rules, and one draw needn't show every extreme that they name: A permutation of the block's positions 0 to 255. `cache_len`: entry s is the number of live slots at the start of sequence group s's 768 cache slots; later slots of that group are not attended. Some group is full.
All inputs are finite; a program needn't handle non-finite values.
Results may differ from a plain program's by a relative error of at most 0.009.
Values may be sent and summed in bfloat16 or wider, within the bound.
A program may use at most 128 MiB of HBM per device.

v0:
```python
from functools import partial

import jax
import jax.numpy as jnp
from jax import lax
from jax.sharding import PartitionSpec as P

DH = 128
GQA = 16


def key_mask(count, query_pos, positions, cache_len, stripe, tok_dev):
    index = jnp.arange(count, dtype=jnp.int32)
    span = stripe + tok_dev
    group = index // span
    offset = index % span
    groups = jnp.arange(cache_len.shape[0], dtype=jnp.int32)
    live_len = jnp.sum(jnp.where(group[:, None] == groups[None, :], cache_len[None, :], 0), axis=1)
    is_cache = offset < stripe
    token = jnp.clip(group * tok_dev + offset - stripe, 0, positions.shape[0] - 1)
    key_pos = jnp.take(positions, token)
    return jnp.where(
        is_cache[None, :], (offset < live_len)[None, :], key_pos[None, :] <= query_pos[:, None]
    )


def softmax_step(
    state, block, begin, query_heads, query_pos, positions, cache_len, stripe, tok_dev
):
    running_max, running_sum, weighted = state
    keys = block[:, :DH]
    values = block[:, DH:]
    scores = jnp.einsum(
        "thd,kd->thk", query_heads, keys, preferred_element_type=jnp.float32
    ) * DH ** (-0.5)
    shown = key_mask(block.shape[0], query_pos, positions, cache_len, stripe, tok_dev)[:, None, :]
    scores = jnp.where(shown, scores, -1e30)
    new_max = jnp.maximum(running_max, jnp.max(scores, axis=2))
    expo = jnp.where(shown, jnp.exp(scores - new_max[:, :, None]), 0.0)
    running_sum = jnp.sum(expo, axis=2)
    weighted = jnp.einsum(
        "thk,kd->thd", expo.astype(jnp.bfloat16), values, preferred_element_type=jnp.float32
    )
    return (new_max, running_sum, weighted)


def empty_state(rows, heads_dev):
    return (
        jnp.full((rows, heads_dev), -1e30, jnp.float32),
        jnp.zeros((rows, heads_dev), jnp.float32),
        jnp.zeros((rows, heads_dev, DH), jnp.float32),
    )


def body(queries, new_keys, new_values, cache_keys, cache_values, positions, cache_len, out_weight):
    tok_dev = queries.shape[0]
    heads_dev = queries.shape[1] // DH
    stripe = cache_keys.shape[0]
    seq_index = lax.axis_index("seq")
    head_index = lax.axis_index("head")
    column = head_index * heads_dev // GQA * DH
    own_keys = jnp.concatenate(
        [
            lax.dynamic_slice_in_dim(cache_keys, column, DH, 1),
            lax.dynamic_slice_in_dim(new_keys, column, DH, 1),
        ],
        axis=0,
    )
    own_values = jnp.concatenate(
        [
            lax.dynamic_slice_in_dim(cache_values, column, DH, 1),
            lax.dynamic_slice_in_dim(new_values, column, DH, 1),
        ],
        axis=0,
    )
    key_block = jnp.concatenate([own_keys, own_values], axis=1)
    query_heads = queries.reshape(tok_dev, heads_dev, DH)
    query_pos = lax.dynamic_slice_in_dim(positions, seq_index * tok_dev, tok_dev)
    stepper = partial(
        softmax_step,
        query_heads=query_heads,
        query_pos=query_pos,
        positions=positions,
        cache_len=cache_len,
        stripe=stripe,
        tok_dev=tok_dev,
    )
    final_max, final_sum, weighted = stepper(
        empty_state(tok_dev, heads_dev),
        lax.all_gather(key_block, "seq", axis=0, tiled=True),
        jnp.int32(0),
    )
    attended = (
        (weighted / final_sum[:, :, None]).astype(jnp.bfloat16).reshape(tok_dev, heads_dev * DH)
    )
    partial_out = jnp.dot(
        lax.all_gather(attended, "seq", axis=0, tiled=True),
        out_weight,
        preferred_element_type=jnp.float32,
    )
    return lax.psum(partial_out, "head")


def solution(mesh):
    placed = (
        P("seq", "head"),
        P("seq", None),
        P("seq", None),
        P("seq", None),
        P("seq", None),
        P(),
        P(),
        P("head", "seq"),
    )
    return jax.shard_map(
        body, mesh=mesh, in_specs=placed, out_specs=P(None, "seq"), check_vma=False
    )
```

profile of v0, /device:TPU:0, one launch (start us, length us, event | category | flops | bytes accessed | tf_op | source)
XLA Modules:
  0.0 214.3 jit_solution(2551049296829856070)
XLA Ops:
  6.5 0.0 copy-start
  6.5 0.0 copy-start.1
  6.5 0.0 all-gather.2.cloned.1.call-start
  6.5 0.8 constant_dynamic-slice_fusion
  7.3 1.0 constant_dynamic-slice_fusion.1
  8.4 0.8 maximum_maximum_fusion
  9.2 0.0 all-gather.2.cloned.1.call-update
  9.2 0.0 all-reduce.2.cloned.1.call-start
  9.3 0.8 dynamic_slice.15
  10.0 0.1 fusion.28
  10.1 0.0 copy-done.1
  10.2 0.0 copy-start.3
  10.2 19.9 %gather_fusion = s32[3328]{0:T(1024)S(1)} fusion(s32[256]{0:T(256)S(1)} %copy-done.1, s32[4096]{0:T(1024)S(1)} %pad_clamp_fusion), kind=kCustom, calls=%fused_computation | custom fusion | bytes 39936 | tf_op jit(solution)/shard_map/jit(_take)/gather | solution.py:21
  30.1 0.0 copy-done.3
  30.1 0.1 select_reduce_fusion
  30.3 0.2 compare_select_fusion
  30.5 2.0 all-gather.2.cloned.1.call-done
  32.4 0.0 copy-done
  32.4 0.0 copy-start.4
  32.5 2.2 %fusion.33 = (f32[64,4]{0,1:T(4,128)S(1)}, f32[64,4,3328]{2,0,1:T(8,128)S(1)}) fusion(bf16[3328,256]{1,0:T(8,128)(2,1)} %all-gather.2.cloned.1.call-done, pred[64,3328]{1,0:T(8,128)(4,1)S(1)} %compare_select_fusion, bf16[64,512]{1,0:T(8,128)(2,1)S(1)} %copy-done), kind=kOutput, calls=%fused_computation.55 | convolution fusion | flops 220659456 | bytes 4539392 | tf_op jit(solution)/shard_map/thd,kd->thk/dot_general | solution.py:33
  34.6 0.8 fusion.2
  35.5 0.0 copy-done.4
  35.5 0.0 copy-start.2
  35.5 0.8 fusion.15
  36.3 5.9 %all_gather.7 = bf16[256,512]{1,0:T(8,128)(2,1)S(1)} all-gather(bf16[64,512]{1,0:T(8,128)(2,1)S(1)} %bitcast.28), channel_id=1, replica_groups=mesh['seq'=4,'head'=8] {'seq'}, dimensions={0}, use_global_device_ids=true | all-gather | bytes 327680 | tf_op jit(solution)/shard_map/all_gather | solution.py:97
  42.2 0.0 copy-done.2
  42.2 3.3 %fusion.34 = f32[256,4096]{1,0:T(8,128)} fusion(bf16[256,512]{1,0:T(8,128)(2,1)S(1)} %all_gather.7, bf16[512,4096]{1,0:T(8,128)(2,1)S(1)} %copy-done.2), kind=kOutput, calls=%fused_computation.56 | convolution fusion | flops 1073741824 | bytes 8650752 | tf_op jit(solution)/shard_map/dot_general | solution.py:96
  45.5 0.0 all-reduce.2.cloned.1.call-update
  45.5 157.3 %all-reduce.2.cloned.1.call-done = f32[256,4096]{1,0:T(8,128)} async-done(((f32[256,4096]{1,0:T(8,128)}), f32[256,4096]{1,0:T(8,128)}) %all-reduce.2.cloned.1.call-update) | async-done | bytes 4194320 | tf_op jit(solution)/shard_map/psum | solution.py:101
  202.8 4.7 %copy.25 = f32[256,4096]{1,0:T(8,128)} copy(f32[256,4096]{1,0:T(8,128)} %all-reduce.2.cloned.1.call-done) | data formatting | bytes 8388608
  (6 shorter events, 0.1 us)
Async XLA Ops:
  6.5 25.9 %copy-start = (bf16[64,512]{1,0:T(8,128)(2,1)S(1)}, bf16[64,512]{1,0:T(8,128)(2,1)}, u32[]{:S(2)}) copy-start(bf16[64,512]{1,0:T(8,128)(2,1)} %param.8) | copy-start | bytes 196612
  6.5 3.6 %copy-start.1 = (s32[256]{0:T(256)S(1)}, s32[256]{0:T(256)}, u32[]{:S(2)}) copy-start(s32[256]{0:T(256)} %param.13) | copy-start | bytes 3076
  6.5 25.9 %all-gather.2.cloned.1.call-start = ((), (), s32[]{:S(2)}) async-start(), calls=%async_computation | async-start | bytes 2129920 | tf_op jit(solution)/shard_map/all_gather | solution.py:90
  9.2 193.6 %all-reduce.2.cloned.1.call-start = ((), (), s32[]{:S(2)}) async-start(), calls=%async_computation.1 | async-start | bytes 8388608 | tf_op jit(solution)/shard_map/psum | solution.py:101
  10.2 19.9 %copy-start.3 = (s32[4]{0:T(128)S(1)}, s32[4]{0:T(128)}, u32[]{:S(2)}) copy-start(s32[4]{0:T(128)} %param.14) | copy-start | bytes 52
  32.4 3.0 %copy-start.4 = (bf16[3328,256]{1,0:T(8,128)(2,1)S(1)}, bf16[3328,256]{1,0:T(8,128)(2,1)}, u32[]{:S(2)}) copy-start(bf16[3328,256]{1,0:T(8,128)(2,1)} %all-gather.2.cloned.1.call-done) | copy-start | bytes 5111812
  35.5 6.8 %copy-start.2 = (bf16[512,4096]{1,0:T(8,128)(2,1)S(1)}, bf16[512,4096]{1,0:T(8,128)(2,1)}, u32[]{:S(2)}) copy-start(bf16[512,4096]{1,0:T(8,128)(2,1)} %param.15) | copy-start | bytes 12582916
Sparse Core Ops, SparseCore 0:
  9.3 23.0 all-gather.1
  45.7 157.1 all-reduce.1
where the time goes:
time: 215 us; the launch traced here: 214 us
  waiting for transfers between devices  159 us (74%)
  local copies, waits for them, and re-layouts  27.2 us (13%)
  between operations  13.5 us (6%)
  matrix products  6.27 us (3%)
  blocking collectives  5.91 us (3%)
  other arithmetic  2.15 us (1%)
    psum x1, waiting for transfers between devices, body(): return lax.psum(partial_out, 'head')  157 us
    gather x1, local copies, waits for them, and re-layouts, key_mask(): key_pos = jnp.take(positions, token)  19.9 us
    all_gather x1, blocking collectives, body(): lax.all_gather(attended, 'seq', axis=0, tiled=True)  5.91 us
    unnamed x11, local copies, waits for them, and re-layouts  4.67 us
  transfers between devices with their start and end apart: 2, of which 2 were waited for; matrix products, arithmetic and copies ran while one was open for 10% of the time, Pallas kernels for 0%

commit v1 on v0

v1 whole, which is shorter than its diff:
```python
from functools import partial

import jax
import jax.numpy as jnp
from jax import lax
from jax.experimental import pallas as pl
from jax.experimental.pallas import tpu as pltpu
from jax.sharding import PartitionSpec as P

DH = 128
GQA = 16
MESH = pl.DeviceIdType.MESH
HIDDEN = -1e30


def kernel(
    n_seq, n_head, groups,
    q_ref, ck_ref, nk_ref, cv_ref, nv_ref, pos_ref, len_ref, w_hbm,
    out_ref,
    w_ref, k_ref, v_ref, q_all, o_send, o_recv, t_send, t_recv, att,
    y_send, y_recv, z_send, z_recv, own, fin,
    w_sem, q_s, q_r, o_s, o_r, t_s, t_r, a_s, a_r,
    y_s, y_r, z_s, z_r, f_s, f_r, g_s, g_r,
):
    f32, bf16 = jnp.float32, jnp.bfloat16
    me = lax.axis_index("seq")
    head = lax.axis_index("head")
    n_out = n_head // 2
    y = lax.rem(head, 2)
    z = head // 2
    mate = z * 2 + (1 - y)
    tok, width = q_ref.shape
    heads = width // DH
    stripe = ck_ref.shape[0]
    total = n_seq * tok
    cols = w_hbm.shape[1]
    wide = cols // groups
    half = wide // 2
    rows = total // n_out

    w_copy = pltpu.make_async_copy(w_hbm, w_ref, w_sem)
    w_copy.start()

    def seq_id(d):
        return lax.rem(me + d, n_seq)

    def z_id(d):
        return lax.rem(z + d, n_out)

    barrier = pltpu.get_barrier_semaphore()
    for d in range(1, n_seq):
        pl.semaphore_signal(barrier, inc=1, device_id=(seq_id(d), head), device_id_type=MESH)
    for d in range(1, n_out):
        pl.semaphore_signal(barrier, inc=1, device_id=(me, z_id(d) * 2 + y), device_id_type=MESH)
    pl.semaphore_signal(barrier, inc=1, device_id=(me, mate), device_id_type=MESH)
    pl.semaphore_wait(barrier, n_seq + n_out - 1)

    def remote(src, dst, ss, rs, device):
        return pltpu.make_async_remote_copy(
            src_ref=src, dst_ref=dst, send_sem=ss, recv_sem=rs, device_id=device, device_id_type=MESH
        )

    sends = []

    def send(src, dst, ss, rs, device):
        copy = remote(src, dst, ss, rs, device)
        copy.start()
        sends.append(copy)

    def arrive(dst, ss, rs, device):
        remote(dst, dst, ss, rs, device).wait_recv()

    for d in range(1, n_seq):
        p = seq_id(d)
        send(q_ref, q_all.at[me], q_s.at[p], q_r.at[me], (p, head))

    column = pl.multiple_of(head * heads // GQA * DH, DH)
    k_ref[:stripe] = ck_ref[:, pl.ds(column, DH)]
    k_ref[stripe:] = nk_ref[:, pl.ds(column, DH)]
    v_ref[:stripe] = cv_ref[:, pl.ds(column, DH)]
    v_ref[stripe:] = nv_ref[:, pl.ds(column, DH)]

    pos_row = pos_ref[...].astype(f32)

    def token_pos(b):
        pick = lax.broadcasted_iota(jnp.int32, (tok, total), 0) + b * tok
        lane = lax.broadcasted_iota(jnp.int32, (tok, total), 1)
        return jnp.sum(jnp.where(pick == lane, pos_row, 0.0), axis=1, keepdims=True)

    eye = lax.broadcasted_iota(jnp.int32, (tok, tok), 0) == lax.broadcasted_iota(
        jnp.int32, (tok, tok), 1
    )
    own_row = jnp.sum(jnp.where(eye, token_pos(me), 0.0), axis=0, keepdims=True)
    live = lax.broadcasted_iota(jnp.int32, (1, stripe), 1) < len_ref[me]
    key_row = jnp.concatenate([jnp.where(live, -1.0, 1e9), own_row], axis=1)
    scale = DH ** (-0.5)

    def attend(block, b):
        stacked = jnp.concatenate([block[:, h * DH : (h + 1) * DH] for h in range(heads)], axis=0)
        scores = lax.dot_general(
            stacked, k_ref[...], (((1,), (1,)), ((), ())), preferred_element_type=f32
        ) * scale
        shown = key_row <= token_pos(b)
        scores = jnp.concatenate(
            [
                jnp.where(shown, scores[h * tok : (h + 1) * tok], HIDDEN)
                for h in range(heads)
            ],
            axis=0,
        )
        peak = jnp.max(scores, axis=1, keepdims=True)
        expo = jnp.exp(scores - peak)
        weight = jnp.sum(expo, axis=1, keepdims=True)
        mixed = jnp.dot(expo.astype(bf16), v_ref[...], preferred_element_type=f32) / weight
        level = peak + jnp.log(weight)
        lane = lax.broadcasted_iota(jnp.int32, (tok, DH), 1)
        stats = jnp.zeros((tok, DH), f32)
        for h in range(heads):
            stats = jnp.where(lane == h, level[h * tok : (h + 1) * tok], stats)
        mixed = jnp.concatenate([mixed[h * tok : (h + 1) * tok] for h in range(heads)], axis=1)
        return mixed, stats

    own_mixed, own_stats = attend(q_ref[...], me)
    for d in range(1, n_seq):
        p = seq_id(d)
        arrive(q_all.at[p], q_s.at[p], q_r.at[p], (p, head))
        mixed, stats = attend(q_all[p], p)
        o_send[p] = mixed.astype(bf16)
        t_send[p] = stats
        send(t_send.at[p], t_recv.at[me], t_s.at[p], t_r.at[me], (p, head))
        send(o_send.at[p], o_recv.at[me], o_s.at[p], o_r.at[me], (p, head))

    for d in range(1, n_seq):
        p = seq_id(d)
        arrive(t_recv.at[p], t_s.at[p], t_r.at[p], (p, head))
    top = own_stats
    for d in range(1, n_seq):
        top = jnp.maximum(top, t_recv[seq_id(d)])

    def spread(share):
        return jnp.concatenate(
            [jnp.broadcast_to(share[:, h : h + 1], (tok, DH)) for h in range(heads)], axis=1
        )

    share = jnp.exp(own_stats - top)
    norm = share
    mixed = own_mixed * spread(share)
    for d in range(1, n_seq):
        p = seq_id(d)
        arrive(o_recv.at[p], o_s.at[p], o_r.at[p], (p, head))
        share = jnp.exp(t_recv[p] - top)
        norm = norm + share
        mixed = mixed + o_recv[p].astype(f32) * spread(share)
    att[me] = (mixed / spread(norm)).astype(bf16)

    for d in range(1, n_seq):
        p = seq_id(d)
        send(att.at[me], att.at[me], a_s.at[p], a_r.at[me], (p, head))
    for d in range(1, n_seq):
        p = seq_id(d)
        arrive(att.at[p], a_s.at[p], a_r.at[p], (p, head))
    w_copy.wait()

    def project(g, side):
        begin = pl.multiple_of(g * wide + side * half, 128)
        return jnp.dot(
            att[...].reshape(total, width), w_ref[:, pl.ds(begin, half)], preferred_element_type=f32
        )

    for g in range(groups):
        y_send[g] = project(g, 1 - y).astype(bf16)
        send(y_send.at[g], y_recv.at[g], y_s.at[g], y_r.at[g], (me, mate))
    for g in range(groups):
        mine = project(g, y)
        arrive(y_recv.at[g], y_s.at[g], y_r.at[g], (me, mate))
        summed = mine + y_recv[g].astype(f32)
        z_send[g] = summed.astype(bf16).reshape(n_out, rows, half)
        own[g] = summed.reshape(n_out, rows, half)
        for d in range(1, n_out):
            p = z_id(d)
            send(z_send.at[g, p], z_recv.at[g, z], z_s.at[g, p], z_r.at[g, z], (me, p * 2 + y))
    for g in range(groups):
        result = own[g, z]
        for d in range(1, n_out):
            p = z_id(d)
            arrive(z_recv.at[g, p], z_s.at[g, p], z_r.at[g, p], (me, p * 2 + y))
            result = result + z_recv[g, p].astype(f32)
        fin[g, y, z] = result.astype(bf16)
        for d in range(1, n_out):
            p = z_id(d)
            send(fin.at[g, y, z], fin.at[g, y, z], f_s.at[g, p], f_r.at[g, z], (me, p * 2 + y))
        send(fin.at[g, y, z], fin.at[g, y, z], g_s.at[g, z], g_r.at[g, z], (me, mate))

    def place(g, side, r):
        begin = pl.multiple_of(g * wide + side * half, 128)
        out_ref[pl.ds(pl.multiple_of(r * rows, rows), rows), pl.ds(begin, half)] = fin[g, side, r]

    for g in range(groups):
        place(g, y, z)
        for d in range(1, n_out):
            p = z_id(d)
            arrive(fin.at[g, y, p], f_s.at[g, p], f_r.at[g, p], (me, p * 2 + y))
            send(fin.at[g, y, p], fin.at[g, y, p], g_s.at[g, p], g_r.at[g, p], (me, mate))
            place(g, y, p)
    for g in range(groups):
        for d in range(n_out):
            p = z_id(d)
            arrive(fin.at[g, 1 - y, p], g_s.at[g, p], g_r.at[g, p], (me, mate))
            place(g, 1 - y, p)
    for copy in sends:
        copy.wait_send()


def body(n_seq, n_head, queries, new_keys, new_values, cache_keys, cache_values, positions, cache_len, out_weight):
    tok, width = queries.shape
    stripe = cache_keys.shape[0]
    depth, cols = out_weight.shape
    total = n_seq * tok
    n_out = n_head // 2
    groups = max(1, min(4, cols // 256))
    half = cols // groups // 2
    rows = total // n_out
    bf16, f32 = jnp.bfloat16, jnp.float32
    vmem = pl.BlockSpec(memory_space=pltpu.VMEM)
    dma = pltpu.SemaphoreType.DMA
    out = pl.pallas_call(
        partial(kernel, n_seq, n_head, groups),
        out_shape=jax.ShapeDtypeStruct((total, cols), bf16),
        in_specs=[vmem] * 6
        + [pl.BlockSpec(memory_space=pltpu.SMEM), pl.BlockSpec(memory_space=pl.ANY)],
        out_specs=vmem,
        scratch_shapes=[
            pltpu.VMEM((depth, cols), bf16),
            pltpu.VMEM((stripe + tok, DH), bf16),
            pltpu.VMEM((stripe + tok, DH), bf16),
            pltpu.VMEM((n_seq, tok, width), bf16),
            pltpu.VMEM((n_seq, tok, width), bf16),
            pltpu.VMEM((n_seq, tok, width), bf16),
            pltpu.VMEM((n_seq, tok, DH), f32),
            pltpu.VMEM((n_seq, tok, DH), f32),
            pltpu.VMEM((n_seq, tok, width), bf16),
            pltpu.VMEM((groups, total, half), bf16),
            pltpu.VMEM((groups, total, half), bf16),
            pltpu.VMEM((groups, n_out, rows, half), bf16),
            pltpu.VMEM((groups, n_out, rows, half), bf16),
            pltpu.VMEM((groups, n_out, rows, half), f32),
            pltpu.VMEM((groups, 2, n_out, rows, half), bf16),
            dma,
        ]
        + [dma((n_seq,))] * 8
        + [dma((groups,))] * 2
        + [dma((groups, n_out))] * 6,
        compiler_params=pltpu.CompilerParams(
            collective_id=0, has_side_effects=True, vmem_limit_bytes=48 * 1024 * 1024
        ),
    )(
        queries, cache_keys, new_keys, cache_values, new_values,
        positions.reshape(1, total), cache_len, out_weight,
    )
    return out.astype(f32)


def solution(mesh):
    placed = (
        P("seq", "head"),
        P("seq", None),
        P("seq", None),
        P("seq", None),
        P("seq", None),
        P(),
        P(),
        P("head", "seq"),
    )
    return jax.shard_map(
        partial(body, mesh.shape["seq"], mesh.shape["head"]),
        mesh=mesh, in_specs=placed, out_specs=P(None, "seq"), check_vma=False,
    )
```

time: 215 us -> 91 us (0.42)
  waiting for transfers between devices: 159 us -> 0 us
  Pallas kernels: 0 us -> 81.6 us
  local copies, waits for them, and re-layouts: 27.2 us -> 5.68 us
  between operations: 13.5 us -> 0.02 us
  matrix products: 6.27 us -> 0 us
  blocking collectives: 5.91 us -> 0 us
    psum x1 -> x0, waiting for transfers between devices: 157 us -> none  [body(): return lax.psum(partial_out, 'head')]
    pallas_call x0 -> x1, Pallas kernels: none -> 81.6 us  [body(): pl.pallas_call(partial(kernel, n_seq, n_head, groups), out_shape=jax.Shap...]
    gather x1 -> x0, local copies, waits for them, and re-layouts: 19.9 us -> none  [key_mask(): key_pos = jnp.take(positions, token)]
    dot_general x3 -> x0, matrix products: 6.27 us -> none  [the longest x1 3.27 us: body(): jnp.dot(lax.all_gather(attended, 'seq', axis=0, tiled=True), out_weight,...]
    all_gather x1 -> x0, blocking collectives: 5.91 us -> none  [body(): lax.all_gather(attended, 'seq', axis=0, tiled=True)]
    dynamic_slice x3 -> x0, local copies, waits for them, and re-layouts: 2.58 us -> none  [the longest x1 1.05 us: body(): lax.dynamic_slice_in_dim(cache_values, column, DH, 1)]
    convert_element_type x0 -> x1, other arithmetic: none -> 2.5 us  [body(): return out.astype(f32)]
    unnamed x11 -> x14, local copies, waits for them, and re-layouts: 4.67 us -> 5.68 us
  transfers between devices with their start and end apart: 2 -> 0, of which waited for: 2 -> 0; matrix products, arithmetic and copies ran while one was open for 10% -> 0% of each run, Pallas kernels for 0% -> 0%
where the time goes in v1:
time: 91 us; the launch traced here: 89.8 us
  Pallas kernels  81.6 us (90%)
  local copies, waits for them, and re-layouts  5.68 us (6%)
  other arithmetic  2.5 us (3%)
    pallas_call x1, Pallas kernels, body(): pl.pallas_call(partial(kernel, n_seq, n_head, groups), out_shape=jax.Shap...  81.6 us
    unnamed x14, local copies, waits for them, and re-layouts  5.68 us
    convert_element_type x1, other arithmetic, body(): return out.astype(f32)  2.5 us

profile of v1, /device:TPU:0, one launch (start us, length us, event | category | flops | bytes accessed | tf_op | source)
XLA Modules:
  0.0 89.8 jit_solution(12971604450318191202)
XLA Ops:
  0.0 0.0 copy-start
  0.0 1.0 %copy-done = bf16[768,256]{1,0:T(8,128)(2,1)S(1)} copy-done((bf16[768,256]{1,0:T(8,128)(2,1)S(1)}, bf16[768,256]{1,0:T(8,128)(2,1)}, u32[]{:S(2)}) %copy-start) | copy-done | bytes 393240
  1.0 0.0 copy-start.1
  1.0 1.0 %copy-done.1 = bf16[768,256]{1,0:T(8,128)(2,1)S(1)} copy-done((bf16[768,256]{1,0:T(8,128)(2,1)S(1)}, bf16[768,256]{1,0:T(8,128)(2,1)}, u32[]{:S(2)}) %copy-start.1) | copy-done | bytes 393240
  2.0 0.0 copy-start.2
  2.0 0.8 copy-done.2
  2.8 0.0 copy-start.3
  2.8 0.8 copy-done.3
  3.6 0.0 copy-start.4
  3.6 0.8 copy-done.4
  4.3 0.0 copy-start.5
  4.4 0.7 copy-done.5
  5.0 0.0 copy-start.6
  5.0 0.7 copy-done.6
  5.7 81.6 %shard_map.82 = bf16[256,4096]{1,0:T(8,128)(2,1)S(1)} custom-call(bf16[64,512]{1,0:T(8,128)(2,1)S(1)} %copy-done.2, bf16[768,256]{1,0:T(8,128)(2,1)S(1)} %copy-done, bf16[64,256]{1,0:T(8,128)(2,1)S(1)} %copy-done.3, bf16[768,256]{1,0:T(8,128)(2,1)S(1)} %copy-done.1, bf16[64,256]{1,0:T(8,128)(2,1)S(1)} %copy-done.4, s32[1,256]{1,0:T(1,128)S(1)} %bitcast.1, ...), custom_call_target="tpu_custom_call" | custom-call | tf_op jit(solution)/shard_map/pallas_call | solution.py:226
  87.3 2.5 %convert_element_type.3 = f32[256,4096]{1,0:T(8,128)} convert(bf16[256,4096]{1,0:T(8,128)(2,1)S(1)} %shard_map.82) | non-fusion elementwise | flops 1048576 | bytes 6291456 | tf_op jit(solution)/shard_map/convert_element_type | solution.py:260
Async XLA Ops:
  0.0 1.0 %copy-start = (bf16[768,256]{1,0:T(8,128)(2,1)S(1)}, bf16[768,256]{1,0:T(8,128)(2,1)}, u32[]{:S(2)}) copy-start(bf16[768,256]{1,0:T(8,128)(2,1)} %ck_ref.1) | copy-start | bytes 1179652
  1.0 1.0 %copy-start.1 = (bf16[768,256]{1,0:T(8,128)(2,1)S(1)}, bf16[768,256]{1,0:T(8,128)(2,1)}, u32[]{:S(2)}) copy-start(bf16[768,256]{1,0:T(8,128)(2,1)} %cv_ref.1) | copy-start | bytes 1179652
  2.0 0.8 copy-start.2
  2.8 0.8 copy-start.3
  3.6 0.8 copy-start.4
  4.3 0.7 copy-start.5
  5.0 0.7 copy-start.6

commit v2 on v1

--- a/solution.py
+++ b/solution.py
@@ -14,13 +14,14 @@
 
 
 def kernel(
-    n_seq, n_head, groups,
-    q_ref, ck_ref, nk_ref, cv_ref, nv_ref, pos_ref, len_ref, w_hbm,
+    n_seq, n_head, groups, first,
+    q_hbm, ck_hbm, nk_hbm, cv_hbm, nv_hbm, pos_hbm, len_hbm, w_hbm,
     out_ref,
-    w_ref, k_ref, v_ref, q_all, o_send, o_recv, t_send, t_recv, att,
-    y_send, y_recv, z_send, z_recv, own, fin,
-    w_sem, q_s, q_r, o_s, o_r, t_s, t_r, a_s, a_r,
-    y_s, y_r, z_s, z_r, f_s, f_r, g_s, g_r,
+    q_ref, pos_ref, len_ref, w_ref, k_ref, v_ref,
+    q_all, o_send, o_recv, t_send, t_recv, att,
+    y_send, y_recv, own, up_send, up_recv, down_send, down_recv, fin, x_send, x_recv,
+    w_sem, in_sem, q_s, q_r, o_s, o_r, t_s, t_r, a_s, a_r,
+    y_s, y_r, up_s, up_r, down_s, down_r, fup_s, fdown_s, f_r, g_s, g_r, x_s, x_r, h_s, h_r,
 ):
     f32, bf16 = jnp.float32, jnp.bfloat16
     me = lax.axis_index("seq")
@@ -31,13 +32,30 @@
     mate = z * 2 + (1 - y)
     tok, width = q_ref.shape
     heads = width // DH
-    stripe = ck_ref.shape[0]
+    stripe = ck_hbm.shape[0]
     total = n_seq * tok
     cols = w_hbm.shape[1]
     wide = cols // groups
     half = wide // 2
     rows = total // n_out
 
+    column = pl.multiple_of(head * heads // GQA * DH, DH)
+    loads = [
+        pltpu.make_async_copy(src, dst, in_sem.at[i])
+        for i, (src, dst) in enumerate(
+            (
+                (q_hbm, q_ref),
+                (pos_hbm, pos_ref),
+                (len_hbm, len_ref),
+                (ck_hbm.at[:, pl.ds(column, DH)], k_ref.at[pl.ds(0, stripe)]),
+                (nk_hbm.at[:, pl.ds(column, DH)], k_ref.at[pl.ds(stripe, tok)]),
+                (cv_hbm.at[:, pl.ds(column, DH)], v_ref.at[pl.ds(0, stripe)]),
+                (nv_hbm.at[:, pl.ds(column, DH)], v_ref.at[pl.ds(stripe, tok)]),
+            )
+        )
+    ]
+    for copy in loads:
+        copy.start()
     w_copy = pltpu.make_async_copy(w_hbm, w_ref, w_sem)
     w_copy.start()
 
@@ -50,10 +68,20 @@
     barrier = pltpu.get_barrier_semaphore()
     for d in range(1, n_seq):
         pl.semaphore_signal(barrier, inc=1, device_id=(seq_id(d), head), device_id_type=MESH)
-    for d in range(1, n_out):
-        pl.semaphore_signal(barrier, inc=1, device_id=(me, z_id(d) * 2 + y), device_id_type=MESH)
+    above = lax.rem(z + 1, n_out) * 2 + y
+    below = lax.rem(z + n_out - 1, n_out) * 2 + y
     pl.semaphore_signal(barrier, inc=1, device_id=(me, mate), device_id_type=MESH)
-    pl.semaphore_wait(barrier, n_seq + n_out - 1)
+
+    @pl.when(z < n_out - 1)
+    def _():
+        pl.semaphore_signal(barrier, inc=1, device_id=(me, above), device_id_type=MESH)
+
+    @pl.when(z > 0)
+    def _():
+        pl.semaphore_signal(barrier, inc=1, device_id=(me, below), device_id_type=MESH)
+
+    inner = jnp.where(z > 0, 1, 0) + jnp.where(z < n_out - 1, 1, 0)
+    pl.semaphore_wait(barrier, n_seq + inner)
 
     def remote(src, dst, ss, rs, device):
         return pltpu.make_async_remote_copy(
@@ -62,24 +90,23 @@
 
     sends = []
 
+    def post(make, when=None):
+        make().start()
+        sends.append((make, when))
+
     def send(src, dst, ss, rs, device):
-        copy = remote(src, dst, ss, rs, device)
-        copy.start()
-        sends.append(copy)
+        post(lambda: remote(src, dst, ss, rs, device))
 
     def arrive(dst, ss, rs, device):
         remote(dst, dst, ss, rs, device).wait_recv()
 
+    loads[0].wait()
     for d in range(1, n_seq):
         p = seq_id(d)
         send(q_ref, q_all.at[me], q_s.at[p], q_r.at[me], (p, head))
 
-    column = pl.multiple_of(head * heads // GQA * DH, DH)
-    k_ref[:stripe] = ck_ref[:, pl.ds(column, DH)]
-    k_ref[stripe:] = nk_ref[:, pl.ds(column, DH)]
-    v_ref[:stripe] = cv_ref[:, pl.ds(column, DH)]
-    v_ref[stripe:] = nv_ref[:, pl.ds(column, DH)]
-
+    for copy in loads[1:]:
+        copy.wait()
     pos_row = pos_ref[...].astype(f32)
 
     def token_pos(b):
@@ -167,48 +194,178 @@
             att[...].reshape(total, width), w_ref[:, pl.ds(begin, half)], preferred_element_type=f32
         )
 
-    for g in range(groups):
+    def place(g, side, r):
+        begin = pl.multiple_of(g * wide + side * half, 128)
+        out_ref[pl.ds(pl.multiple_of(r * rows, rows), rows), pl.ds(begin, half)] = fin[g, r, side]
+
+    def reduce_step(j, t):
+        rest = n_out - 1 - t
+
+        @pl.when(z == t)
+        def _():
+            if t > 0:
+                arrive(up_recv.at[j, pl.ds(t, rest + 1)], up_s.at[j], up_r.at[j], (me, below))
+                own[j, t] = own[j, t] + up_recv[j, t].astype(f32)
+            if rest > 0:
+                part = own[j, t + 1 :]
+                if t > 0:
+                    part = part + up_recv[j, t + 1 :].astype(f32)
+                up_send[j, t + 1 :] = part.astype(bf16)
+                span = pl.ds(t + 1, rest)
+                post(
+                    lambda: remote(
+                        up_send.at[j, span], up_recv.at[j, span], up_s.at[j], up_r.at[j], (me, above)
+                    ),
+                    lambda: z == t,
+                )
+
+        @pl.when(z == rest)
+        def _():
+            if t > 0:
+                arrive(
+                    down_recv.at[j, pl.ds(0, rest + 1)], down_s.at[j], down_r.at[j], (me, above)
+                )
+                own[j, rest] = own[j, rest] + down_recv[j, rest].astype(f32)
+            if rest > 0:
+                part = own[j, :rest]
+                if t > 0:
+                    part = part + down_recv[j, :rest].astype(f32)
+                down_send[j, :rest] = part.astype(bf16)
+                span = pl.ds(0, rest)
+                post(
+                    lambda: remote(
+                        down_send.at[j, span], down_recv.at[j, span], down_s.at[j], down_r.at[j],
+                        (me, below),
+                    ),
+                    lambda: z == rest,
+                )
+
+    def pass_up(g, j, side, p, when):
+        def make():
+            piece = fin.at[g, p, side]
+            return remote(piece, piece, fup_s.at[j, p], f_r.at[j, p], (me, above))
+
+        pl.when(when())(lambda: post(make, when))
+
+    def pass_down(g, j, side, p, when):
+        def make():
+            piece = fin.at[g, p, side]
+            return remote(piece, piece, fdown_s.at[j, p], f_r.at[j, p], (me, below))
+
+        pl.when(when())(lambda: post(make, when))
+
+    def to_mate(g, p, when=None):
+        def make():
+            piece = fin.at[g, p, y]
+            return remote(piece, piece, g_s.at[g, p], g_r.at[g, p], (me, mate))
+
+        post(make, when)
+
+    def gather_step(g, j, side, t, mated):
+        low, high = z - t, z + t
+
+        @pl.when(low >= 0)
+        def _():
+            arrive(fin.at[g, low, side], fup_s.at[j, low], f_r.at[j, low], (me, below))
+            pass_up(g, j, side, low, lambda: jnp.logical_and(low >= 0, z < n_out - 1))
+            if mated:
+                to_mate(g, low, lambda: low >= 0)
+            place(g, side, low)
+
+        @pl.when(high < n_out)
+        def _():
+            arrive(fin.at[g, high, side], fdown_s.at[j, high], f_r.at[j, high], (me, above))
+            pass_down(g, j, side, high, lambda: jnp.logical_and(high < n_out, z > 0))
+            if mated:
+                to_mate(g, high, lambda: high < n_out)
+            place(g, side, high)
+
+    def open_gather(g, j, side):
+        pass_up(g, j, side, z, lambda: z < n_out - 1)
+        pass_down(g, j, side, z, lambda: z > 0)
+
+    def pair_steps(g):
+        j = g + first
+
+        def begin():
+            summed = project(g, y)
+            arrive(y_recv.at[g], y_s.at[g], y_r.at[g], (me, mate))
+            own[j] = (summed + y_recv[g].astype(f32)).reshape(n_out, rows, half)
+            reduce_step(j, 0)
+
+        def turn():
+            reduce_step(j, n_out - 1)
+            fin[g, z, y] = own[j, z].astype(bf16)
+            open_gather(g, j, y)
+            to_mate(g, z)
+            place(g, y, z)
+
+        def end():
+            for d in range(n_out):
+                p = z_id(d)
+                arrive(fin.at[g, p, 1 - y], g_s.at[g, p], g_r.at[g, p], (me, mate))
+                place(g, 1 - y, p)
+
+        return (
+            [begin]
+            + [partial(reduce_step, j, t) for t in range(1, n_out - 1)]
+            + [turn]
+            + [partial(gather_step, g, j, y, t, True) for t in range(1, n_out)]
+            + [end]
+        )
+
+    def line_steps():
+        def begin():
+            for side in range(2):
+                own[side] = project(0, side).reshape(n_out, rows, half)
+                reduce_step(side, 0)
+
+        def reduce(t):
+            for side in range(2):
+                reduce_step(side, t)
+
+        def swap():
+            reduce(n_out - 1)
+            x_send[...] = own[1 - y, z].astype(bf16)
+            send(x_send, x_recv, x_s, x_r, (me, mate))
+
+        def settle():
+            arrive(x_recv, x_s, x_r, (me, mate))
+            fin[0, z, y] = (own[y, z] + x_recv[...].astype(f32)).astype(bf16)
+            piece = fin.at[0, z, y]
+            send(piece, piece, h_s, h_r, (me, mate))
+            open_gather(0, y, y)
+
+        def turn():
+            arrive(fin.at[0, z, 1 - y], h_s, h_r, (me, mate))
+            open_gather(0, 1 - y, 1 - y)
+            for side in range(2):
+                place(0, side, z)
+
+        def gather(t):
+            for side in range(2):
+                gather_step(0, side, side, t, False)
+
+        return (
+            [begin]
+            + [partial(reduce, t) for t in range(1, n_out - 1)]
+            + [swap, settle, turn]
+            + [partial(gather, t) for t in range(1, n_out)]
+        )
+
+    for g in range(first, groups):
         y_send[g] = project(g, 1 - y).astype(bf16)
         send(y_send.at[g], y_recv.at[g], y_s.at[g], y_r.at[g], (me, mate))
-    for g in range(groups):
-        mine = project(g, y)
-        arrive(y_recv.at[g], y_s.at[g], y_r.at[g], (me, mate))
-        summed = mine + y_recv[g].astype(f32)
-        z_send[g] = summed.astype(bf16).reshape(n_out, rows, half)
-        own[g] = summed.reshape(n_out, rows, half)
-        for d in range(1, n_out):
-            p = z_id(d)
-            send(z_send.at[g, p], z_recv.at[g, z], z_s.at[g, p], z_r.at[g, z], (me, p * 2 + y))
-    for g in range(groups):
-        result = own[g, z]
-        for d in range(1, n_out):
-            p = z_id(d)
-            arrive(z_recv.at[g, p], z_s.at[g, p], z_r.at[g, p], (me, p * 2 + y))
-            result = result + z_recv[g, p].astype(f32)
-        fin[g, y, z] = result.astype(bf16)
-        for d in range(1, n_out):
-            p = z_id(d)
-            send(fin.at[g, y, z], fin.at[g, y, z], f_s.at[g, p], f_r.at[g, z], (me, p * 2 + y))
-        send(fin.at[g, y, z], fin.at[g, y, z], g_s.at[g, z], g_r.at[g, z], (me, mate))
-
-    def place(g, side, r):
-        begin = pl.multiple_of(g * wide + side * half, 128)
-        out_ref[pl.ds(pl.multiple_of(r * rows, rows), rows), pl.ds(begin, half)] = fin[g, side, r]
-
-    for g in range(groups):
-        place(g, y, z)
-        for d in range(1, n_out):
-            p = z_id(d)
-            arrive(fin.at[g, y, p], f_s.at[g, p], f_r.at[g, p], (me, p * 2 + y))
-            send(fin.at[g, y, p], fin.at[g, y, p], g_s.at[g, p], g_r.at[g, p], (me, mate))
-            place(g, y, p)
-    for g in range(groups):
-        for d in range(n_out):
-            p = z_id(d)
-            arrive(fin.at[g, 1 - y, p], g_s.at[g, p], g_r.at[g, p], (me, mate))
-            place(g, 1 - y, p)
-    for copy in sends:
-        copy.wait_send()
+    lines = ([line_steps()] if first else []) + [pair_steps(g) for g in range(first, groups)]
+    for slot in range(max(i + len(steps) for i, steps in enumerate(lines))):
+        for i, steps in enumerate(lines):
+            if 0 <= slot - i < len(steps):
+                steps[slot - i]()
+    for make, when in sends:
+        if when is None:
+            make().wait_send()
+        else:
+            pl.when(when())(lambda: make().wait_send())
 
 
 def body(n_seq, n_head, queries, new_keys, new_values, cache_keys, cache_values, positions, cache_len, out_weight):
@@ -221,15 +378,19 @@
     half = cols // groups // 2
     rows = total // n_out
     bf16, f32 = jnp.bfloat16, jnp.float32
+    first = 1 if groups > 1 else 0
+    chains = groups + first
     vmem = pl.BlockSpec(memory_space=pltpu.VMEM)
     dma = pltpu.SemaphoreType.DMA
     out = pl.pallas_call(
-        partial(kernel, n_seq, n_head, groups),
+        partial(kernel, n_seq, n_head, groups, first),
         out_shape=jax.ShapeDtypeStruct((total, cols), bf16),
-        in_specs=[vmem] * 6
-        + [pl.BlockSpec(memory_space=pltpu.SMEM), pl.BlockSpec(memory_space=pl.ANY)],
+        in_specs=[pl.BlockSpec(memory_space=pl.ANY)] * 8,
         out_specs=vmem,
         scratch_shapes=[
+            pltpu.VMEM((tok, width), bf16),
+            pltpu.VMEM((1, total), jnp.int32),
+            pltpu.SMEM(cache_len.shape, jnp.int32),
             pltpu.VMEM((depth, cols), bf16),
             pltpu.VMEM((stripe + tok, DH), bf16),
             pltpu.VMEM((stripe + tok, DH), bf16),
@@ -241,17 +402,24 @@
             pltpu.VMEM((n_seq, tok, width), bf16),
             pltpu.VMEM((groups, total, half), bf16),
             pltpu.VMEM((groups, total, half), bf16),
-            pltpu.VMEM((groups, n_out, rows, half), bf16),
-            pltpu.VMEM((groups, n_out, rows, half), bf16),
-            pltpu.VMEM((groups, n_out, rows, half), f32),
-            pltpu.VMEM((groups, 2, n_out, rows, half), bf16),
+            pltpu.VMEM((chains, n_out, rows, half), f32),
+        ]
+        + [pltpu.VMEM((chains, n_out, rows, half), bf16)] * 4
+        + [
+            pltpu.VMEM((groups, n_out, 2, rows, half), bf16),
+            pltpu.VMEM((rows, half), bf16),
+            pltpu.VMEM((rows, half), bf16),
             dma,
+            dma((7,)),
         ]
         + [dma((n_seq,))] * 8
         + [dma((groups,))] * 2
-        + [dma((groups, n_out))] * 6,
+        + [dma((chains,))] * 4
+        + [dma((chains, n_out))] * 3
+        + [dma((groups, n_out))] * 2
+        + [dma] * 4,
         compiler_params=pltpu.CompilerParams(
-            collective_id=0, has_side_effects=True, vmem_limit_bytes=48 * 1024 * 1024
+            collective_id=0, has_side_effects=True, vmem_limit_bytes=60 * 1024 * 1024
         ),
     )(
         queries, cache_keys, new_keys, cache_values, new_values,

time: 91 us -> 79 us (0.87); the launches traced: 89.8 us -> 78.9 us
  Pallas kernels: 81.6 us -> 74.8 us
  local copies, waits for them, and re-layouts: 5.68 us -> 0 us
  other arithmetic: 2.5 us -> 4.1 us
    pallas_call x1, Pallas kernels: 81.6 us -> 74.8 us  [body(): pl.pallas_call(partial(kernel, n_seq, n_head, groups, first), out_shape=j...]
    unnamed x14 -> x0, local copies, waits for them, and re-layouts: 5.68 us -> none
    convert_element_type x1, other arithmetic: 2.5 us -> 4.1 us  [body(): return out.astype(f32)]
where the time goes in v2:
time: 79 us; the launch traced here: 78.9 us
  Pallas kernels  74.8 us (95%)
  other arithmetic  4.1 us (5%)
    pallas_call x1, Pallas kernels, body(): pl.pallas_call(partial(kernel, n_seq, n_head, groups, first), out_shape=j...  74.8 us
    convert_element_type x1, other arithmetic, body(): return out.astype(f32)  4.1 us

profile of v2, /device:TPU:0, one launch (start us, length us, event | category | flops | bytes accessed | tf_op | source)
XLA Modules:
  0.0 78.9 jit_solution(7666960857482163120)
XLA Ops:
  0.0 74.8 %shard_map.82 = bf16[256,4096]{1,0:T(8,128)(2,1)} custom-call(bf16[64,512]{1,0:T(8,128)(2,1)} %q_hbm.1, bf16[768,256]{1,0:T(8,128)(2,1)} %ck_hbm.1, bf16[64,256]{1,0:T(8,128)(2,1)} %nk_hbm.1, bf16[768,256]{1,0:T(8,128)(2,1)} %cv_hbm.1, bf16[64,256]{1,0:T(8,128)(2,1)} %nv_hbm.1, s32[1,256]{1,0:T(1,128)} %bitcast.1, s32[4]{0:T(128)} %len_hbm.1, ...), custom_call_target="tpu_custom_call" | custom-call | tf_op jit(solution)/shard_map/pallas_call | solution.py:385
  74.8 4.1 %convert_element_type.3 = f32[256,4096]{1,0:T(8,128)} convert(bf16[256,4096]{1,0:T(8,128)(2,1)} %shard_map.82) | non-fusion elementwise | flops 1048576 | bytes 6291456 | tf_op jit(solution)/shard_map/convert_element_type | solution.py:428
